TPU v7x, 256 devices: a whole 4x4x8 slice. The times are simulated.
256 devices in a mesh: seq: 64 (over z, y, core), head: 4 (over x).
Axes of the slice: x: 4, y: 4, z: 8, core: 2. Of those that a mesh axis runs over, the one named last changes fastest.
Arguments:
- layer_in: bfloat16 [32768, 2048], P('seq', 'head'), may hold values from -6 to 6
- query_weight: bfloat16 [2048, 1024], P(None, 'head'), may hold values from -0.125 to 0.125
- key_weight: bfloat16 [2048, 1024], P(None, 'head'), may hold values from -0.125 to 0.125
- value_weight: bfloat16 [2048, 1024], P(None, 'head'), may hold values from -0.125 to 0.125
- gate_weight: bfloat16 [2048, 1024], P(None, 'head'), may hold values from -0.125 to 0.125
- beta_weight: bfloat16 [2048, 8], P(None, 'head'), may hold values from -0.125 to 0.125
- decay_weight: bfloat16 [2048, 8], P(None, 'head'), may hold values from -0.125 to 0.125
- conv_weight: float32 [4, 3, 1024], P(None, None, 'head'), may hold values from -3 to 3
- decay_log: float32 [8], P('head'), as said below
- beta_bias: float32 [8], P('head'), as said below
- decay_bias: float32 [8], P('head'), may hold values from -1 to 1
- norm_gain: float32 [128], replicated, may hold values from 0.1 to 1.9
- out_weight: bfloat16 [1024, 2048], P('head'), may hold values from -0.1875 to 0.1875
Outputs:
- layer_out: bfloat16 [32768, 2048], P('seq', 'head')
Inputs may be any that keep to these rules, and one draw needn't show every extreme that they name: decay_log lies between log(0.1 / 32768) and log(0.05). beta_bias lies between log(0.5 * 128 / 32768) and 1.
All inputs are finite; a program needn't handle non-finite values.
Results may differ from a plain program's by a relative error of at most 0.0049.
Values may be sent and summed in bfloat16 or wider, within the bound.
A program may use at most 128 MiB of HBM per device.

v0:
```python
import jax
import jax.numpy as jnp
from jax import lax
from jax.sharding import Mesh
from jax.sharding import PartitionSpec as P

BLOCK = 128
SEQ = ("seq_0", "seq_1", "seq_2")
exact_mode = lax.Precision.HIGHEST
norm_floor = 0.0001


def passed_along(value, axis, steps):
    count = lax.axis_size(axis)
    leading, last = (max(0, -steps), min(count, count - steps))
    return lax.ppermute(value, axis, [(source, source + steps) for source in range(leading, last)])


def neutral_like(value, identity):
    return jax.tree.map(
        lambda part, zero: jnp.zeros_like(part) + jnp.asarray(zero, part.dtype), value, identity
    )


def carried_in(value, axes, combine, identity):
    before = start = neutral_like(value, identity)
    subtotal = value
    for axis in reversed(axes):
        length, mine = (lax.axis_size(axis), lax.axis_index(axis))
        pieces = jax.tree.map(lambda part: lax.all_gather(part, axis), subtotal)
        inside, subtotal = (start, start)
        for k in range(length):
            passed = k < mine
            subtotal = combine(subtotal, jax.tree.map(lambda part: part[k], pieces))
            inside = jax.tree.map(lambda new, old: jnp.where(passed, new, old), subtotal, inside)
        before = combine(inside, before)
    return before


def copy_for_each(value, axis):
    length = lax.axis_size(axis)
    return lax.all_to_all(
        jnp.broadcast_to(value[None], (length, *value.shape)), axis, 0, 0, tiled=True
    )


def in_order(tiles, dim):
    tiles = jnp.moveaxis(tiles, 0, dim)
    dims = tiles.shape
    return tiles.reshape(*dims[:dim], dims[dim] * dims[dim + 1], *dims[dim + 2 :])


def collect(value, axis, dim):
    tiles = copy_for_each(value, axis)
    return in_order(tiles, dim)


def causal_conv(values, earlier, kernel):
    reach_back = kernel.shape[0] - 1
    tokens = values.shape[0]
    extended = jnp.concatenate([earlier, values], axis=0)
    summed = kernel[0] * values
    for offset in range(1, reach_back + 1):
        summed = (
            summed + kernel[offset] * extended[reach_back - offset : reach_back - offset + tokens]
        )
    return jax.nn.silu(summed)


def unit_rows(values):
    return values * lax.rsqrt(jnp.sum(values * values, axis=-1, keepdims=True) + 1.0)


def unit_lower_inverse(system):
    length = system.shape[-1]
    row_index = lax.broadcasted_iota(jnp.int32, (length, length), 0)
    col_index = lax.broadcasted_iota(jnp.int32, (length, length), 1)
    inverse = jnp.broadcast_to(jnp.eye(length, dtype=jnp.float32), system.shape)
    width = 1
    while width < length:
        same_pair = row_index // (2 * width) == col_index // (2 * width)
        lower_half = row_index // width > col_index // width
        linking = jnp.where(same_pair & lower_half, system, 0.0)
        middle = lax.optimization_barrier(
            jnp.einsum("...rs,...st->...rt", linking, inverse, precision=exact_mode)
        )
        update = lax.optimization_barrier(
            jnp.einsum("...rs,...st->...rt", inverse, middle, precision=exact_mode)
        )
        inverse = inverse - update
        width = width * 2
    return inverse


def block_terms(queries, key_rows, values, beta_gate, log_decay):
    length = log_decay.shape[-1]
    running = jnp.cumsum(log_decay, axis=-1)
    row_index = lax.broadcasted_iota(jnp.int32, (length, length), 0)
    col_index = lax.broadcasted_iota(jnp.int32, (length, length), 1)
    within = row_index >= col_index
    before = row_index > col_index
    spread = running[..., :, None] - running[..., None, :]
    decay_matrix = jnp.where(within, jnp.exp(jnp.minimum(spread, 0.0)), 0.0)
    key_gram = jnp.einsum("...rd,...sd->...rs", key_rows, key_rows, precision=exact_mode)
    lower_part = jnp.where(before, beta_gate[..., :, None] * decay_matrix * key_gram, 0.0)
    system = lower_part + jnp.eye(length, dtype=jnp.float32)
    growth = jnp.exp(running)
    right_side = jnp.concatenate(
        [beta_gate[..., None] * values, (beta_gate * growth)[..., None] * key_rows], axis=-1
    )
    solved = jnp.einsum(
        "...rs,...se->...re", unit_lower_inverse(system), right_side, precision=exact_mode
    )
    value_dim = values.shape[-1]
    fixed_rows = solved[..., :value_dim]
    erased = solved[..., value_dim:]
    query_key = jnp.einsum("...rd,...sd->...rs", queries, key_rows, precision=exact_mode)
    mixing = jnp.where(within, decay_matrix * query_key, 0.0)
    local_out = jnp.einsum("...rs,...se->...re", mixing, fixed_rows, precision=exact_mode)
    removed = lax.optimization_barrier(
        jnp.einsum("...rs,...sd->...rd", mixing, erased, precision=exact_mode)
    )
    reader = growth[..., None] * queries - removed
    tail_decay = jnp.exp(running[..., -1:] - running)
    weighted = tail_decay[..., None] * key_rows
    key_dim = key_rows.shape[-1]
    lost_part = lax.optimization_barrier(
        jnp.einsum("...bd,...be->...de", weighted, erased, precision=exact_mode)
    )
    transit = (
        jnp.exp(running[..., -1])[..., None, None] * jnp.eye(key_dim, dtype=jnp.float32) - lost_part
    )
    carried = jnp.einsum("...bd,...be->...de", weighted, fixed_rows, precision=exact_mode)
    return (local_out, reader, transit, carried)


def compose(earlier, later_map):
    joined = jnp.einsum("...de,...ef->...df", later_map[0], earlier[0], precision=exact_mode)
    moved = (
        jnp.einsum("...de,...ef->...df", later_map[0], earlier[1], precision=exact_mode)
        + later_map[1]
    )
    return (joined, moved)


def on_device(
    layer_in,
    query_weight,
    key_weight,
    value_weight,
    gate_weight,
    beta_weight,
    decay_weight,
    conv_weight,
    decay_log,
    beta_bias,
    decay_bias,
    norm_gain,
    out_weight,
):
    tokens = layer_in.shape[0]
    head_count = beta_weight.shape[1]
    head_dim = query_weight.shape[1] // head_count
    weights = (query_weight, key_weight, value_weight, gate_weight, beta_weight, decay_weight)
    shard_piece = lax.all_gather(layer_in, "head", axis=1, tiled=True)
    query_raw, key_raw, value_raw, gate_raw, beta_raw, decay_raw = tuple(
        (jnp.dot(shard_piece, weight, preferred_element_type=jnp.float32) for weight in weights)
    )
    reach_back = conv_weight.shape[0] - 1
    channels = query_raw.shape[1]
    last_rows = jnp.concatenate(
        [
            query_raw[tokens - reach_back :],
            key_raw[tokens - reach_back :],
            value_raw[tokens - reach_back :],
        ],
        axis=1,
    )
    prior_rows = passed_along(last_rows, SEQ, 1)
    mixed_query = causal_conv(query_raw, prior_rows[:, :channels], conv_weight[:, 0])
    mixed_key = causal_conv(key_raw, prior_rows[:, channels : 2 * channels], conv_weight[:, 1])
    mixed_value = causal_conv(value_raw, prior_rows[:, 2 * channels :], conv_weight[:, 2])
    queries = unit_rows(mixed_query.reshape(tokens, head_count, head_dim))
    key_rows = unit_rows(mixed_key.reshape(tokens, head_count, head_dim))
    values = mixed_value.reshape(tokens, head_count, head_dim)
    beta_gate = jax.nn.sigmoid(beta_raw + beta_bias)
    log_decay = -jnp.exp(decay_log) * jax.nn.softplus(decay_raw + decay_bias)
    blocks = tokens // BLOCK

    def arrange(array):
        return array.reshape(blocks, BLOCK, head_count, head_dim).transpose(0, 2, 1, 3)

    def arrange_gate(array):
        return array.reshape(blocks, BLOCK, head_count).transpose(0, 2, 1)

    local_out, reader, transit, carried = block_terms(
        arrange(queries),
        arrange(key_rows),
        arrange(values),
        arrange_gate(beta_gate),
        arrange_gate(log_decay),
    )
    identity = jnp.broadcast_to(
        jnp.eye(head_dim, dtype=jnp.float32), (head_count, head_dim, head_dim)
    )
    nothing = jnp.zeros((head_count, head_dim, head_dim), jnp.float32)

    def through(running_pair, block_maps):
        return (compose(running_pair, block_maps), None)

    slab_pair, unused_rest = lax.scan(through, (identity, nothing), (transit, carried))
    slab_transit, slab_state = slab_pair
    scanned = carried_in((slab_transit, slab_state), SEQ, compose, (identity, nothing))
    incoming = scanned[1]

    def advance(carry_state, block_maps):
        following = (
            jnp.einsum("hde,hef->hdf", block_maps[0], carry_state, precision=exact_mode)
            + block_maps[1]
        )
        return (following, carry_state)

    unused_last, starts = lax.scan(advance, incoming, (transit, carried))
    outputs = local_out + jnp.einsum("nhrd,nhde->nhre", reader, starts, precision=exact_mode)
    head_out = outputs.transpose(0, 2, 1, 3).reshape(tokens, head_count, head_dim)
    gate_rows = gate_raw.reshape(tokens, head_count, head_dim)
    scaled = head_out * lax.rsqrt(
        jnp.mean(head_out * head_out, axis=-1, keepdims=True) + norm_floor
    )
    hidden = (
        (scaled * norm_gain * jax.nn.silu(gate_rows))
        .reshape(tokens, head_count * head_dim)
        .astype(jnp.bfloat16)
    )
    column_weight = lax.all_to_all(out_weight, "head", split_axis=1, concat_axis=0, tiled=True)
    summed = jnp.dot(collect(hidden, "head", 1), column_weight, preferred_element_type=jnp.float32)
    return summed.astype(jnp.bfloat16)


def solution(mesh):
    finer = Mesh(
        mesh.devices.reshape(8, 4, 2, mesh.shape["head"]), ("seq_0", "seq_1", "seq_2", "head")
    )
    return jax.shard_map(
        on_device,
        mesh=finer,
        in_specs=(
            P(SEQ, "head"),
            P(None, "head"),
            P(None, "head"),
            P(None, "head"),
            P(None, "head"),
            P(None, "head"),
            P(None, "head"),
            P(None, None, "head"),
            P("head"),
            P("head"),
            P("head"),
            P(),
            P("head", None),
        ),
        out_specs=P(SEQ, "head"),
        check_vma=False,
    )
```

profile of v0, /device:TPU:8, one launch (start us, length us, event | category | flops | bytes accessed | tf_op | source)
XLA Modules:
  0.0 231.8 jit_solution(16035866141420245483)
XLA Ops:
  6.5 0.7 all-gather.10.cloned.1.call-update
  7.5 1.2 exponential_negate_fusion
  8.7 1.5 fusion.183
  10.7 34.6 %all-gather.10.cloned.1.call-done = bf16[512,2048]{1,0:T(8,128)(2,1)} async-done(((bf16[512,512]{1,0:T(8,128)(2,1)}), bf16[512,2048]{1,0:T(8,128)(2,1)}) %all-gather.10.cloned.1.call-update) | async-done | bytes 2097168 | tf_op jit(solution)/shard_map/all_gather | solution.py:165
  45.4 2.4 %fusion.166 = f32[4,2,128]{2,1,0:T(2,128)S(1)} fusion(bf16[512,2048]{1,0:T(8,128)(2,1)} %all-gather.10.cloned.1.call-done, bf16[2048,2]{0,1:T(2,128)(2,1)} %param.23, f32[2]{0:T(128)} %param.27, f32[2]{0:T(128)} %exponential_negate_fusion), kind=kOutput, calls=%fused_computation.232 | convolution fusion | flops 4202496 | bytes 2109456 | tf_op jit(solution)/shard_map/dot_general | solution.py:167
  47.8 1.2 reduce_window_sum.11
  49.3 0.7 fusion.188
  50.5 0.7 fusion.187
  51.3 0.8 copy-done.38
  52.1 0.7 fusion.186
  52.8 2.1 collective-permute-start
  55.0 0.7 fusion.185
  55.7 2.1 collective-permute-done
  57.8 1.9 fusion.182
  61.1 1.4 fusion.17
  63.7 0.7 fusion.75
  64.4 0.7 fusion.87
  65.1 0.7 fusion.73
  66.5 0.7 fusion.71
  67.9 0.7 fusion.69
  69.3 0.7 fusion.67
  70.8 0.9 fusion.65
  71.7 1.5 fusion.193
  73.1 1.1 bitcast_multiply_fusion.3
  74.3 1.6 fusion.181
  76.4 2.2 fusion.26
  78.7 1.3 fusion.79
  80.0 1.3 fusion.80
  81.4 2.4 %while.28 = (s32[]{:T(128)}, f32[2,128,128]{2,1,0:T(8,128)S(1)}, f32[2,128,128]{2,1,0:T(8,128)S(1)}, f32[4,2,128,128]{3,2,1,0:T(8,128)S(1)}, f32[4,2,128,128]{3,2,1,0:T(8,128)S(1)}) while((s32[]{:T(128)}, f32[2,128,128]{2,1,0:T(8,128)S(1)}, f32[2,128,128]{2,1,0:T(8,128)S(1)}, f32[4,2,128,128]{3,2,1,0:T(8,128)S(1)}, ...), condition=%wide.region_4.5_spmd.clone.clone, body=%wide.region_3.4_spmd.clone.sunk.clone | while | flops 100728832 | bytes 1443410 | solution.py:211
  85.2 2.2 all-gather
  88.3 13.5 %all-gather.1 = f32[8,128,128]{2,1,0:T(8,128)S(1)} all-gather(f32[2,128,128]{2,1,0:T(8,128)S(1)} %fusion.195), channel_id=3, replica_groups=mesh['seq_0'=8,'seq_1'=4,'seq_2'=2,'head'=4] {'seq_1'}, dimensions={0}, use_global_device_ids=true | all-gather | bytes 655360 | tf_op jit(solution)/shard_map/all_gather | solution.py:30
  104.6 0.9 fusion.198
  105.6 2.3 copy.83
  107.8 2.3 copy.84
  110.1 4.2 %all-to-all-start.1 = ((bf16[256,4,512]{2,0,1:T(8,128)(2,1)}), bf16[256,4,512]{2,0,1:T(8,128)(2,1)}, u32[]{:S(2)}, u32[]{:S(2)}) async-start(bf16[256,4,512]{2,0,1:T(8,128)(2,1)} %copy.84), calls=%async_computation.1 | async-start | bytes 2097152 | tf_op jit(solution)/shard_map/all_to_all | solution.py:235
  114.4 2.2 all-gather.3
  117.8 13.5 %all-gather.4 = f32[8,128,128]{2,1,0:T(8,128)S(1)} all-gather(f32[2,128,128]{2,1,0:T(8,128)S(1)} %convolution_add_fusion.13), channel_id=6, replica_groups=mesh['seq_0'=8,'seq_1'=4,'seq_2'=2,'head'=4] {'seq_1'}, dimensions={0}, use_global_device_ids=true | all-gather | bytes 655360 | tf_op jit(solution)/shard_map/all_gather | solution.py:30
  133.1 0.9 convolution_add_fusion.10
  134.2 2.2 mul.279
  136.3 2.4 %reduce_sum.27 = f32[512,2]{1,0:T(8,128)} reduce(f32[512,2,128]{2,1,0:T(2,128)} %mul.279, f32[]{:T(128)} %constant.233.clone.1), dimensions={2}, to_apply=%region_1.2 | reduce | flops 130048 | bytes 528388 | tf_op jit(solution)/shard_map/reduce_sum | solution.py:71
  138.7 1.0 add_rsqrt_fusion.1
  139.8 2.2 reshape.130
  142.0 2.5 %fusion.18 = f32[4,2,128,128]{3,2,1,0:T(8,128)S(1)} fusion(f32[4,128,2,128]{3,2,1,0:T(2,128)} %reshape.130, f32[4,128,2,128]{3,2,1,0:T(2,128)S(1)} %copy-done.2, f32[4,128,2]{1,2,0:T(2,128)S(1)} %bitcast.192, f32[4,128,2]{1,2,0:T(2,128)S(1)} %bitcast.193, f32[4,2,128]{2,1,0:T(2,128)S(1)} %reduce_window_sum.11, pred[128,128]{1,0:T(8,128)(4,1)S(1)} %get-tuple-element.135), kind=kOutput, calls=%fused_computation.25 | convolution fusion | flops 202244096 | bytes 1601536 | tf_op jit(solution)/shard_map/...rd,...sd->...rs/dot_general | solution.py:117
  144.5 1.5 fusion.82
  147.0 1.8 fusion.85
  148.8 35.7 %all-gather.14.cloned.1.call-done = f32[16,128,128]{2,1,0:T(8,128)} async-done(((f32[2,128,128]{2,1,0:T(8,128)}), f32[16,128,128]{2,1,0:T(8,128)}) %all-gather.14.cloned.1.call-update) | async-done | bytes 1048592 | tf_op jit(solution)/shard_map/all_gather | solution.py:30
  184.5 1.3 convolution_add_fusion.16
  185.8 1.2 convolution_add_fusion.9
  187.1 1.2 convolution_add_fusion.8
  188.3 1.2 convolution_add_fusion.7
  191.2 7.5 %while.27 = (s32[]{:T(128)}, f32[2,128,128]{2,1,0:T(8,128)S(1)}, f32[4,2,128,128]{3,2,1,0:T(8,128)}, f32[4,2,128,128]{3,2,1,0:T(8,128)S(1)}, f32[4,2,128,128]{3,2,1,0:T(8,128)}) while((s32[]{:T(128)}, f32[2,128,128]{2,1,0:T(8,128)S(1)}, f32[4,2,128,128]{3,2,1,0:T(8,128)}, f32[4,2,128,128]{3,2,1,0:T(8,128)S(1)}, ...), condition=%wide.region_6.7_spmd.clone, body=%wide.region_5.6_spmd.sunk.clone | while | flops 50364416 | bytes 1049673 | solution.py:223
  191.2 0.7 bitcast_dynamic-update-slice_fusion.3
  191.9 1.2 convolution_add_fusion.24
  193.1 0.7 bitcast_dynamic-update-slice_fusion.3
  193.8 1.2 convolution_add_fusion.24
  195.0 0.7 bitcast_dynamic-update-slice_fusion.3
  195.7 1.2 convolution_add_fusion.24
  196.9 0.7 bitcast_dynamic-update-slice_fusion.3
  197.6 1.2 convolution_add_fusion.24
  198.7 3.8 %multiply_reduce_fusion = (f32[4,128,2]{1,2,0:T(2,128)S(1)}, f32[4,128,2,128]{1,3,2,0:T(8,128)}) fusion(f32[4,2,128,128]{2,3,1,0:T(8,128)} %fusion.85, f32[4,2,128,128]{3,2,1,0:T(8,128)} %get-tuple-element.62, f32[4,2,128,128]{3,2,1,0:T(8,128)} %fusion.82, f32[4,128,2,128]{3,2,1,0:T(2,128)} %reshape.130, f32[4,2,128]{2,1,0:T(2,128)S(1)} %get-tuple-element.120, ...), kind=kOutput, calls=%fused_computation.103 | convolution fusion | flops 202112000 | bytes 2633728 | tf_op jit(solution)/shard_map/nhrd,nhde->nhre/dot_general | solution.py:224
  202.7 2.0 copy.81
  205.4 2.1 fusion.55
  207.6 14.9 %all_to_all.21 = bf16[4,512,256]{2,1,0:T(8,128)(2,1)S(1)} all-to-all(bf16[4,512,256]{2,1,0:T(8,128)(2,1)S(1)} %broadcast_in_dim.110), channel_id=1, replica_groups=mesh['seq_0'=8,'seq_1'=4,'seq_2'=2,'head'=4] {'head'}, dimensions={0} | all-to-all | bytes 2097152 | tf_op jit(solution)/shard_map/all_to_all | solution.py:42
  222.5 2.7 %fusion.14 = bf16[512,512]{1,0:T(8,128)(2,1)} fusion(bf16[256,4,512]{2,0,1:T(8,128)(2,1)} %all-to-all-done.1, bf16[4,512,256]{2,1,0:T(8,128)(2,1)S(1)} %all_to_all.21), kind=kOutput, calls=%fused_computation.18 | convolution fusion | flops 537133056 | bytes 2621440 | tf_op jit(solution)/shard_map/dot_general | solution.py:236
  (200 shorter events, 21.3 us)
Async XLA Ops:
  6.5 42.8 %copy-start = (bf16[2048,256]{1,0:T(8,128)(2,1)S(1)}, bf16[2048,256]{1,0:T(8,128)(2,1)}, u32[]{:S(2)}) copy-start(bf16[2048,256]{1,0:T(8,128)(2,1)} %param.20) | copy-start | bytes 3145732
  6.5 38.8 %all-gather.10.cloned.1.call-start = ((), (), s32[]{:S(2)}) async-start(), calls=%async_computation.2 | async-start | bytes 2621440 | tf_op jit(solution)/shard_map/all_gather | solution.py:165
  7.3 141.5 %all-gather.12.cloned.1.call-start = ((), (), s32[]{:S(2)}) async-start(), calls=%async_computation.3 | async-start | bytes 1179648 | tf_op jit(solution)/shard_map/all_gather | solution.py:30
  45.4 3.9 %copy-start.5 = (bf16[512,2048]{1,0:T(8,128)(2,1)S(1)}, bf16[512,2048]{1,0:T(8,128)(2,1)}, u32[]{:S(2)}) copy-start(bf16[512,2048]{1,0:T(8,128)(2,1)} %all-gather.10.cloned.1.call-done) | copy-start | bytes 6291460
  49.3 1.2 copy-start.48
  50.0 2.8 %copy-start.34 = (f32[512,256]{1,0:T(8,128)}, f32[512,256]{1,0:T(8,128)S(1)}, u32[]{:S(2)}) copy-start(f32[512,256]{1,0:T(8,128)S(1)} %fusion.188) | copy-start | bytes 1572868
  50.0 2.0 copy-start.49
  51.2 0.8 copy-start.38
  52.0 2.9 %copy-start.39 = (bf16[2048,2]{0,1:T(2,128)(2,1)S(1)}, bf16[2048,2]{0,1:T(2,128)(2,1)}, u32[]{:S(2)}) copy-start(bf16[2048,2]{0,1:T(2,128)(2,1)} %param.22) | copy-start | bytes 24580
  52.0 2.9 %copy-start.47 = (f32[2]{0:T(128)S(1)}, f32[2]{0:T(128)}, u32[]{:S(2)}) copy-start(f32[2]{0:T(128)} %param.26) | copy-start | bytes 28
  52.8 2.8 %copy-start.36 = (f32[512,256]{1,0:T(8,128)}, f32[512,256]{1,0:T(8,128)S(1)}, u32[]{:S(2)}) copy-start(f32[512,256]{1,0:T(8,128)S(1)} %fusion.186) | copy-start | bytes 1572868
  52.8 5.0 %collective-permute-start = (f32[3,768]{1,0:T(4,128)S(1)}, f32[3,768]{1,0:T(4,128)S(1)}, u32[]{:S(2)}, u32[]{:S(2)}) collective-permute-start(f32[3,768]{1,0:T(4,128)S(1)} %pad_maximum_fusion.3), channel_id=1, source_target_pairs={{0,4},{4,8},{8,12},{12,16},{16,20},{20,24},{24,28},{28,32},{32,36}... | collective-permute-start | bytes 27656 | tf_op jit(solution)/shard_map/ppermute | solution.py:16
  61.1 18.9 %copy-start.1 = (f32[4,128,2,128]{3,2,1,0:T(2,128)}, f32[4,128,2,128]{3,2,1,0:T(2,128)S(1)}, u32[]{:S(2)}) copy-start(f32[4,128,2,128]{3,2,1,0:T(2,128)S(1)} %reshape.131) | copy-start | bytes 1572868
  70.7 3.6 %copy-start.3 = (f32[4,2,128,128]{3,2,1,0:T(8,128)}, f32[4,2,128,128]{3,2,1,0:T(8,128)S(1)}, u32[]{:S(2)}) copy-start(f32[4,2,128,128]{3,2,1,0:T(8,128)S(1)} %sub.166) | copy-start | bytes 1572868
  70.7 3.6 %copy-start.35 = (f32[512,256]{1,0:T(8,128)S(1)}, f32[512,256]{1,0:T(8,128)}, u32[]{:S(2)}) copy-start(f32[512,256]{1,0:T(8,128)} %copy-done.34) | copy-start | bytes 1572868
  70.7 3.6 %copy-start.37 = (f32[512,256]{1,0:T(8,128)S(1)}, f32[512,256]{1,0:T(8,128)}, u32[]{:S(2)}) copy-start(f32[512,256]{1,0:T(8,128)} %copy-done.36) | copy-start | bytes 1572868
  70.7 3.6 %copy-start.40 = (f32[1,1,256]{2,0,1:T(1,128)S(1)}, f32[1,1,256]{2,0,1:T(1,128)}, u32[]{:S(2)}) copy-start(f32[1,1,256]{2,0,1:T(1,128)} %get-tuple-element.106) | copy-start | bytes 3076
  70.7 3.6 %copy-start.41 = (f32[1,1,256]{2,0,1:T(1,128)S(1)}, f32[1,1,256]{2,0,1:T(1,128)}, u32[]{:S(2)}) copy-start(f32[1,1,256]{2,0,1:T(1,128)} %get-tuple-element.111) | copy-start | bytes 3076
  70.7 3.6 %copy-start.42 = (f32[1,1,256]{2,0,1:T(1,128)S(1)}, f32[1,1,256]{2,0,1:T(1,128)}, u32[]{:S(2)}) copy-start(f32[1,1,256]{2,0,1:T(1,128)} %get-tuple-element.112) | copy-start | bytes 3076
  70.7 3.6 %copy-start.43 = (f32[1,1,256]{2,0,1:T(1,128)S(1)}, f32[1,1,256]{2,0,1:T(1,128)}, u32[]{:S(2)}) copy-start(f32[1,1,256]{2,0,1:T(1,128)} %get-tuple-element.113) | copy-start | bytes 3076
  70.7 3.6 %copy-start.44 = (f32[1,1,256]{2,0,1:T(1,128)S(1)}, f32[1,1,256]{2,0,1:T(1,128)}, u32[]{:S(2)}) copy-start(f32[1,1,256]{2,0,1:T(1,128)} %get-tuple-element.114) | copy-start | bytes 3076
  70.7 3.6 %copy-start.45 = (f32[1,1,256]{2,0,1:T(1,128)S(1)}, f32[1,1,256]{2,0,1:T(1,128)}, u32[]{:S(2)}) copy-start(f32[1,1,256]{2,0,1:T(1,128)} %get-tuple-element.115) | copy-start | bytes 3076
  70.8 3.6 %copy-start.46 = (f32[1,1,256]{2,0,1:T(1,128)S(1)}, f32[1,1,256]{2,0,1:T(1,128)}, u32[]{:S(2)}) copy-start(f32[1,1,256]{2,0,1:T(1,128)} %get-tuple-element.116) | copy-start | bytes 3076
  74.3 2.1 copy-start.4
  83.9 0.6 copy-start.9
  84.5 0.7 copy-start.10
  85.2 2.5 %copy-start.8 = (f32[4,2,128,128]{3,2,1,0:T(8,128)}, f32[4,2,128,128]{3,2,1,0:T(8,128)S(1)}, u32[]{:S(2)}) copy-start(f32[4,2,128,128]{3,2,1,0:T(8,128)S(1)} %get-tuple-element.279) | copy-start | bytes 1572868
  87.6 0.7 copy-start.15
  88.3 13.5 %copy-start.17 = (f32[2,128,128]{2,1,0:T(8,128)}, f32[2,128,128]{2,1,0:T(8,128)S(1)}, u32[]{:S(2)}) copy-start(f32[2,128,128]{2,1,0:T(8,128)S(1)} %fusion.195) | copy-start | bytes 393220
  102.1 0.7 copy-start.21
  103.0 0.7 copy-start.23
  104.0 0.7 copy-start.25
  110.1 97.4 %all-to-all-start.1 = ((bf16[256,4,512]{2,0,1:T(8,128)(2,1)}), bf16[256,4,512]{2,0,1:T(8,128)(2,1)}, u32[]{:S(2)}, u32[]{:S(2)}) async-start(bf16[256,4,512]{2,0,1:T(8,128)(2,1)} %copy.84), calls=%async_computation.1 | async-start | bytes 2097152 | tf_op jit(solution)/shard_map/all_to_all | solution.py:235
  114.4 70.2 %all-gather.14.cloned.1.call-start = ((), (), s32[]{:S(2)}) async-start(), calls=%async_computation.4 | async-start | bytes 1179648 | tf_op jit(solution)/shard_map/all_gather | solution.py:30
  116.9 0.7 copy-start.13
  117.5 16.6 %copy-start.50 = (f32[128]{0:T(128)S(1)}, f32[128]{0:T(128)}, u32[]{:S(2)}) copy-start(f32[128]{0:T(128)} %param.28) | copy-start | bytes 1540
  117.8 14.3 %copy-start.11 = (f32[2,128,128]{2,1,0:T(8,128)}, f32[2,128,128]{2,1,0:T(8,128)S(1)}, u32[]{:S(2)}) copy-start(f32[2,128,128]{2,1,0:T(8,128)S(1)} %convolution_add_fusion.13) | copy-start | bytes 393220
  131.6 0.7 copy-start.27
  131.9 0.6 copy-start.29
  132.5 0.6 copy-start.31
  134.1 7.9 %copy-start.2 = (f32[4,128,2,128]{3,2,1,0:T(2,128)S(1)}, f32[4,128,2,128]{3,2,1,0:T(2,128)}, u32[]{:S(2)}) copy-start(f32[4,128,2,128]{3,2,1,0:T(2,128)} %copy-done.1) | copy-start | bytes 1572868
  139.8 6.2 %copy-start.16 = (f32[2,128,128]{2,1,0:T(8,128)S(1)}, f32[2,128,128]{2,1,0:T(8,128)}, u32[]{:S(2)}) copy-start(f32[2,128,128]{2,1,0:T(8,128)} %copy-done.15) | copy-start | bytes 393220
  139.8 6.2 %copy-start.18 = (f32[2,128,128]{2,1,0:T(8,128)S(1)}, f32[2,128,128]{2,1,0:T(8,128)}, u32[]{:S(2)}) copy-start(f32[2,128,128]{2,1,0:T(8,128)} %copy-done.17) | copy-start | bytes 393220
  142.0 4.3 %copy-start.20 = (f32[2,128,128]{2,1,0:T(8,128)S(1)}, f32[2,128,128]{2,1,0:T(8,128)}, u32[]{:S(2)}) copy-start(f32[2,128,128]{2,1,0:T(8,128)} %convolution_add_fusion.10) | copy-start | bytes 393220
  142.0 4.4 %copy-start.28 = (f32[2,128,128]{2,1,0:T(8,128)S(1)}, f32[2,128,128]{2,1,0:T(8,128)}, u32[]{:S(2)}) copy-start(f32[2,128,128]{2,1,0:T(8,128)} %copy-done.27) | copy-start | bytes 393220
  142.0 4.4 %copy-start.30 = (f32[2,128,128]{2,1,0:T(8,128)S(1)}, f32[2,128,128]{2,1,0:T(8,128)}, u32[]{:S(2)}) copy-start(f32[2,128,128]{2,1,0:T(8,128)} %copy-done.29) | copy-start | bytes 393220
  142.0 4.4 %copy-start.32 = (f32[2,128,128]{2,1,0:T(8,128)S(1)}, f32[2,128,128]{2,1,0:T(8,128)}, u32[]{:S(2)}) copy-start(f32[2,128,128]{2,1,0:T(8,128)} %copy-done.31) | copy-start | bytes 393220
  142.0 4.7 %copy-start.19 = (f32[2,128,128]{2,1,0:T(8,128)S(1)}, f32[2,128,128]{2,1,0:T(8,128)}, u32[]{:S(2)}) copy-start(f32[2,128,128]{2,1,0:T(8,128)} %fusion.198) | copy-start | bytes 393220
  142.0 4.7 %copy-start.22 = (f32[2,128,128]{2,1,0:T(8,128)S(1)}, f32[2,128,128]{2,1,0:T(8,128)}, u32[]{:S(2)}) copy-start(f32[2,128,128]{2,1,0:T(8,128)} %copy-done.21) | copy-start | bytes 393220
  142.0 4.7 %copy-start.24 = (f32[2,128,128]{2,1,0:T(8,128)S(1)}, f32[2,128,128]{2,1,0:T(8,128)}, u32[]{:S(2)}) copy-start(f32[2,128,128]{2,1,0:T(8,128)} %copy-done.23) | copy-start | bytes 393220
  142.0 4.7 %copy-start.26 = (f32[2,128,128]{2,1,0:T(8,128)S(1)}, f32[2,128,128]{2,1,0:T(8,128)}, u32[]{:S(2)}) copy-start(f32[2,128,128]{2,1,0:T(8,128)} %copy-done.25) | copy-start | bytes 393220
  148.8 39.5 %copy-start.7 = (f32[16,128,128]{2,1,0:T(8,128)S(1)}, f32[16,128,128]{2,1,0:T(8,128)}, u32[]{:S(2)}) copy-start(f32[16,128,128]{2,1,0:T(8,128)} %all-gather.12.cloned.1.call-done) | copy-start | bytes 3145732
  184.5 5.0 %copy-start.33 = (f32[16,128,128]{2,1,0:T(8,128)S(1)}, f32[16,128,128]{2,1,0:T(8,128)}, u32[]{:S(2)}) copy-start(f32[16,128,128]{2,1,0:T(8,128)} %all-gather.14.cloned.1.call-done) | copy-start | bytes 3145732
  189.5 1.4 copy-start.12
  189.5 1.4 copy-start.14
  198.7 6.7 %copy-start.6 = (bf16[512,2048]{1,0:T(8,128)(2,1)S(1)}, bf16[512,2048]{1,0:T(8,128)(2,1)}, u32[]{:S(2)}) copy-start(bf16[512,2048]{1,0:T(8,128)(2,1)} %all-gather.10.cloned.1.call-done) | copy-start | bytes 6291460
Sparse Core Ops, SparseCore 0:
  9.1 36.1 all-gather.9
  105.7 40.1 all-gather.11
  147.7 36.7 all-gather.13
where the time goes:
time: 233 us; the launch traced here: 232 us
  waiting for transfers between devices  73.2 us (31%)
  matrix products  54.7 us (23%)
  blocking collectives  46.3 us (20%)
  local copies, waits for them, and re-layouts  24.2 us (10%)
  between operations  14.3 us (6%)
  other arithmetic  12.4 us (5%)
  starting transfers between devices  6.43 us (3%)
    all_gather x2, waiting for transfers between devices, carried_in(): pieces = jax.tree.map(lambda part: lax.all_gather(part, axis), subtotal)  35.7 us
    all_gather x1, waiting for transfers between devices, on_device(): shard_piece = lax.all_gather(layer_in, 'head', axis=1, tiled=True)  34.6 us
    all_gather x4, blocking collectives, carried_in(): pieces = jax.tree.map(lambda part: lax.all_gather(part, axis), subtotal)  31.4 us
    all_to_all x1, blocking collectives, copy_for_each(): lax.all_to_all(jnp.broadcast_to(value[None], (length, *value.shape)), axi...  14.9 us
    dot_general x21, matrix products, compose(): jnp.einsum('...de,...ef->...df', later_map[0], earlier[1], precision=exac...  10.1 us
    unnamed x105, local copies, waits for them, and re-layouts  9.2 us
    dot_general x6, matrix products, on_device(): jnp.dot(shard_piece, weight, preferred_element_type=jnp.float32)  7.33 us
    dot_general x7, matrix products, unit_lower_inverse(): jnp.einsum('...rs,...st->...rt', inverse, middle, precision=exact_mode)  5.3 us
  transfers between devices with their start and end apart: 5, of which 3 were waited for; matrix products, arithmetic and copies ran while one was open for 21% of the time, Pallas kernels for 0%

commit v1 on v0

--- a/solution.py
+++ b/solution.py
@@ -162,7 +162,10 @@
     head_count = beta_weight.shape[1]
     head_dim = query_weight.shape[1] // head_count
     weights = (query_weight, key_weight, value_weight, gate_weight, beta_weight, decay_weight)
-    shard_piece = lax.all_gather(layer_in, "head", axis=1, tiled=True)
+    size = lax.axis_size("head")
+    parts = jnp.stack([layer_in for _ in range(size)])
+    parts = lax.all_to_all(parts, "head", split_axis=0, concat_axis=0)
+    shard_piece = jnp.concatenate(parts, axis=1)
     query_raw, key_raw, value_raw, gate_raw, beta_raw, decay_raw = tuple(
         (jnp.dot(shard_piece, weight, preferred_element_type=jnp.float32) for weight in weights)
     )

time: 233 us -> 240 us (1.030); the launches traced: 232 us -> 235 us
  waiting for transfers between devices: 73.2 us -> 67 us
  local copies, waits for them, and re-layouts: 24.2 us -> 30.1 us
  starting transfers between devices: 6.43 us -> 11 us
  matrix products: 54.7 us -> 51.5 us
    all_gather x1 -> x0, waiting for transfers between devices: 34.6 us -> none  [on_device(): shard_piece = lax.all_gather(layer_in, 'head', axis=1, tiled=True)]
    all_to_all x0 -> x1, waiting for transfers between devices: none -> 23.1 us  [on_device(): parts = lax.all_to_all(parts, 'head', split_axis=0, concat_axis=0)]
    reshape x0 -> x4, local copies, waits for them, and re-layouts: none -> 9.86 us  [the longest x3 7.8 us: on_device(): shard_piece = jnp.concatenate(parts, axis=1)]
    all_gather x2, waiting for transfers between devices: 35.7 us -> 43.9 us  [carried_in(): pieces = jax.tree.map(lambda part: lax.all_gather(part, axis), subtotal)]
    all_to_all x0 -> x1, starting transfers between devices: none -> 4.42 us  [on_device(): parts = lax.all_to_all(parts, 'head', split_axis=0, concat_axis=0)]
    unnamed x105 -> x113, local copies, waits for them, and re-layouts: 9.2 us -> 5.47 us
    another operation x0 -> x1, local copies, waits for them, and re-layouts: none -> 2.6 us  [on_device(): parts = jnp.stack([layer_in for _ in range(size)])]
  transfers between devices with their start and end apart: 5 -> 5, of which waited for: 3 -> 3; matrix products, arithmetic and copies ran while one was open for 21% -> 24% of each run, Pallas kernels for 0% -> 0%
where the time goes in v1:
time: 240 us; the launch traced here: 235 us
  waiting for transfers between devices  67 us (28%)
  matrix products  51.5 us (21%)
  blocking collectives  46.8 us (20%)
  local copies, waits for them, and re-layouts  30.1 us (13%)
  between operations  14.9 us (6%)
  other arithmetic  13.8 us (6%)
  starting transfers between devices  11 us (5%)
    all_gather x2, waiting for transfers between devices, carried_in(): pieces = jax.tree.map(lambda part: lax.all_gather(part, axis), subtotal)  43.9 us
    all_gather x4, blocking collectives, carried_in(): pieces = jax.tree.map(lambda part: lax.all_gather(part, axis), subtotal)  31.8 us
    all_to_all x1, waiting for transfers between devices, on_device(): parts = lax.all_to_all(parts, 'head', split_axis=0, concat_axis=0)  23.1 us
    all_to_all x1, blocking collectives, copy_for_each(): lax.all_to_all(jnp.broadcast_to(value[None], (length, *value.shape)), axi...  14.9 us
    dot_general x21, matrix products, compose(): jnp.einsum('...de,...ef->...df', later_map[0], earlier[1], precision=exac...  10.9 us
    reshape x3, local copies, waits for them, and re-layouts, on_device(): shard_piece = jnp.concatenate(parts, axis=1)  7.8 us
    dot_general x6, matrix products, on_device(): jnp.dot(shard_piece, weight, preferred_element_type=jnp.float32)  7.31 us
    unnamed x113, local copies, waits for them, and re-layouts  5.47 us
  transfers between devices with their start and end apart: 5, of which 3 were waited for; matrix products, arithmetic and copies ran while one was open for 24% of the time, Pallas kernels for 0%

profile of v1, /device:TPU:8, one launch (start us, length us, event | category | flops | bytes accessed | tf_op | source)
XLA Modules:
  0.0 235.3 jit_solution(13354847335281367759)
XLA Ops:
  6.5 2.6 %stack.2 = bf16[4,512,512]{2,1,0:T(8,128)(2,1)} broadcast(bf16[512,512]{1,0:T(8,128)(2,1)} %param.17), dimensions={1,2} | broadcast | bytes 2621440 | tf_op jit(solution)/shard_map/stack | solution.py:166
  9.1 4.4 %all-to-all-start = ((bf16[4,512,512]{2,1,0:T(8,128)(2,1)}), bf16[4,512,512]{2,1,0:T(8,128)(2,1)S(1)}, u32[]{:S(2)}, u32[]{:S(2)}) async-start(bf16[4,512,512]{2,1,0:T(8,128)(2,1)} %stack.2), calls=%async_computation | async-start | bytes 4194304 | tf_op jit(solution)/shard_map/all_to_all | solution.py:167
  15.6 1.1 fusion.142
  16.8 23.1 %all-to-all-done = bf16[4,512,512]{2,1,0:T(8,128)(2,1)S(1)} async-done(((bf16[4,512,512]{2,1,0:T(8,128)(2,1)}), bf16[4,512,512]{2,1,0:T(8,128)(2,1)S(1)}, u32[]{:S(2)}, u32[]{:S(2)}) %all-to-all-start) | async-done | bytes 2097184 | tf_op jit(solution)/shard_map/all_to_all | solution.py:167
  40.2 1.0 copy-done.1
  41.2 0.7 fusion.183
  42.0 1.2 copy-done.51
  43.2 0.7 fusion.184
  44.0 0.7 fusion.185
  44.8 1.9 collective-permute-start
  46.8 0.7 fusion.163
  47.5 1.7 reduce_window_sum.11
  49.4 2.3 fusion.182
  53.6 1.4 fusion.17
  56.1 0.7 fusion.72
  63.1 0.8 fusion.62
  64.6 1.2 bitcast_multiply_fusion.2
  65.8 1.6 fusion.178
  67.4 1.1 reshape_reshape.3
  68.5 1.2 bitcast_multiply_fusion
  69.7 2.1 fusion.26
  71.8 1.3 fusion.76
  73.1 1.3 fusion.77
  74.6 2.4 %while.28 = (s32[]{:T(128)}, f32[2,128,128]{2,1,0:T(8,128)S(1)}, f32[2,128,128]{2,1,0:T(8,128)S(1)}, f32[4,2,128,128]{3,2,1,0:T(8,128)S(1)}, f32[4,2,128,128]{3,2,1,0:T(8,128)S(1)}) while((s32[]{:T(128)}, f32[2,128,128]{2,1,0:T(8,128)S(1)}, f32[2,128,128]{2,1,0:T(8,128)S(1)}, f32[4,2,128,128]{3,2,1,0:T(8,128)S(1)}, ...), condition=%wide.region_4.5_spmd.clone.clone, body=%wide.region_3.4_spmd.clone.sunk.clone | while | flops 100728832 | bytes 1442891 | solution.py:214
  77.0 3.3 %all-gather = f32[4,128,128]{2,1,0:T(8,128)S(1)} all-gather(f32[2,128,128]{2,1,0:T(8,128)S(1)} %get-tuple-element.60), channel_id=2, replica_groups=mesh['seq_0'=8,'seq_1'=4,'seq_2'=2,'head'=4] {'seq_2'}, dimensions={0}, use_global_device_ids=true | all-gather | bytes 393216 | tf_op jit(solution)/shard_map/all_gather | solution.py:30
  80.3 2.0 all-gather.3
  83.1 13.7 %all-gather.4 = f32[8,128,128]{2,1,0:T(8,128)S(1)} all-gather(f32[2,128,128]{2,1,0:T(8,128)S(1)} %convolution_add_fusion.13), channel_id=6, replica_groups=mesh['seq_0'=8,'seq_1'=4,'seq_2'=2,'head'=4] {'seq_1'}, dimensions={0}, use_global_device_ids=true | all-gather | bytes 655360 | tf_op jit(solution)/shard_map/all_gather | solution.py:30
  97.1 12.8 %all-gather.1 = f32[8,128,128]{2,1,0:T(8,128)S(1)} all-gather(f32[2,128,128]{2,1,0:T(8,128)S(1)} %fusion.192), channel_id=3, replica_groups=mesh['seq_0'=8,'seq_1'=4,'seq_2'=2,'head'=4] {'seq_1'}, dimensions={0}, use_global_device_ids=true | all-gather | bytes 655360 | tf_op jit(solution)/shard_map/all_gather | solution.py:30
  111.1 0.9 convolution_add_fusion.10
  113.0 0.9 fusion.195
  114.0 1.5 copy.65
  115.5 1.3 copy.66
  116.8 4.6 %all-to-all-start.2 = ((bf16[256,4,512]{2,0,1:T(8,128)(2,1)}), bf16[256,4,512]{2,0,1:T(8,128)(2,1)}, u32[]{:S(2)}, u32[]{:S(2)}) async-start(bf16[256,4,512]{2,0,1:T(8,128)(2,1)} %copy.66), calls=%async_computation.2 | async-start | bytes 2097152 | tf_op jit(solution)/shard_map/all_to_all | solution.py:238
  121.4 2.3 copy.69
  123.8 3.0 %copy.46 = bf16[512,4,512]{2,1,0:T(4,128)(2,1)} copy(bf16[512,4,512]{2,0,1:T(8,128)(2,1)S(1)} %bitcast.178) | data formatting | bytes 4194304 | tf_op jit(solution)/shard_map/reshape | solution.py:168
  126.7 4.5 %reshape.209 = bf16[512,2048,1]{1,0,2:T(8,128)(2,1)} reshape(bf16[512,4,512]{2,1,0:T(4,128)(2,1)} %copy.46) | data formatting | bytes 4194304 | tf_op jit(solution)/shard_map/reshape | solution.py:168
  131.3 1.1 mul.269
  132.3 2.5 %reduce_sum.27 = f32[512,2]{1,0:T(8,128)} reduce(f32[512,2,128]{2,1,0:T(2,128)} %mul.269, f32[]{:T(128)} %constant.233.clone.1), dimensions={2}, to_apply=%region_1.2 | reduce | flops 130048 | bytes 528388 | tf_op jit(solution)/shard_map/reduce_sum | solution.py:71
  134.8 1.7 add_rsqrt_fusion.1
  136.5 1.1 copy.71
  137.6 1.1 reshape.143
  138.7 2.5 %fusion.18 = f32[4,2,128,128]{3,2,1,0:T(8,128)S(1)} fusion(f32[4,128,2,128]{3,2,1,0:T(2,128)} %reshape.143, f32[4,128,2,128]{3,2,1,0:T(2,128)S(1)} %copy-done.8, f32[4,128,2]{1,2,0:T(2,128)S(1)} %bitcast.193, f32[4,128,2]{1,2,0:T(2,128)S(1)} %bitcast.194, f32[4,2,128]{2,1,0:T(2,128)S(1)} %reduce_window_sum.11, pred[128,128]{1,0:T(8,128)(4,1)S(1)} %get-tuple-element.135), kind=kOutput, calls=%fused_computation.25 | convolution fusion | flops 202244096 | bytes 1601536 | tf_op jit(solution)/shard_map/...rd,...sd->...rs/dot_general | solution.py:117
  142.2 0.9 fusion.117
  143.2 0.9 fusion.122
  144.8 5.3 %all-gather.11.cloned.1.call-done = f32[16,128,128]{2,1,0:T(8,128)} async-done(((f32[2,128,128]{2,1,0:T(8,128)}), f32[16,128,128]{2,1,0:T(8,128)}) %all-gather.11.cloned.1.call-update) | async-done | bytes 1048592 | tf_op jit(solution)/shard_map/all_gather | solution.py:30
  150.0 38.6 %all-gather.9.cloned.1.call-done = f32[16,128,128]{2,1,0:T(8,128)} async-done(((f32[2,128,128]{2,1,0:T(8,128)}), f32[16,128,128]{2,1,0:T(8,128)}) %all-gather.9.cloned.1.call-update) | async-done | bytes 1048592 | tf_op jit(solution)/shard_map/all_gather | solution.py:30
  188.6 1.4 convolution_add_fusion.16
  190.0 1.2 convolution_add_fusion.9
  191.3 1.2 convolution_add_fusion.8
  192.5 1.2 convolution_add_fusion.7
  195.4 7.7 %while.27 = (s32[]{:T(128)}, f32[2,128,128]{2,1,0:T(8,128)S(1)}, f32[4,2,128,128]{3,2,1,0:T(8,128)}, f32[4,2,128,128]{3,2,1,0:T(8,128)}, f32[4,2,128,128]{3,2,1,0:T(8,128)}) while((s32[]{:T(128)}, f32[2,128,128]{2,1,0:T(8,128)S(1)}, f32[4,2,128,128]{3,2,1,0:T(8,128)}, f32[4,2,128,128]{3,2,1,0:T(8,128)}, ...), condition=%wide.region_6.7_spmd.clone, body=%wide.region_5.6_spmd.sunk.clone | while | flops 50364416 | bytes 1050173 | solution.py:226
  195.5 0.7 bitcast_dynamic-update-slice_fusion.3
  196.1 1.2 convolution_add_fusion.24
  198.1 1.2 convolution_add_fusion.24
  199.3 0.7 bitcast_dynamic-update-slice_fusion.3
  200.0 1.2 convolution_add_fusion.24
  201.3 0.7 bitcast_dynamic-update-slice_fusion.3
  201.9 1.2 convolution_add_fusion.24
  203.2 2.0 multiply_reduce_fusion
  205.2 0.8 copy.61
  206.1 2.1 copy.62
  208.2 2.2 multiply_convert_fusion
  210.6 14.9 %all_to_all.26 = bf16[4,512,256]{2,1,0:T(8,128)(2,1)S(1)} all-to-all(bf16[4,512,256]{2,1,0:T(8,128)(2,1)S(1)} %broadcast_in_dim.110), channel_id=1, replica_groups=mesh['seq_0'=8,'seq_1'=4,'seq_2'=2,'head'=4] {'head'}, dimensions={0} | all-to-all | bytes 2097152 | tf_op jit(solution)/shard_map/all_to_all | solution.py:42
  225.5 2.7 %fusion.14 = bf16[512,512]{1,0:T(8,128)(2,1)} fusion(bf16[256,4,512]{2,0,1:T(8,128)(2,1)} %all-to-all-done.2, bf16[4,512,256]{2,1,0:T(8,128)(2,1)S(1)} %all_to_all.26), kind=kOutput, calls=%fused_computation.18 | convolution fusion | flops 537133056 | bytes 2621440 | tf_op jit(solution)/shard_map/dot_general | solution.py:239
  (211 shorter events, 22.1 us)
Async XLA Ops:
  6.5 34.7 %copy-start = (bf16[2048,256]{1,0:T(8,128)(2,1)S(1)}, bf16[2048,256]{1,0:T(8,128)(2,1)}, u32[]{:S(2)}) copy-start(bf16[2048,256]{1,0:T(8,128)(2,1)} %param.18) | copy-start | bytes 3145732
  9.1 5.1 %copy-start.53 = (f32[2]{0:T(128)S(1)}, f32[2]{0:T(128)}, u32[]{:S(2)}) copy-start(f32[2]{0:T(128)} %param.25) | copy-start | bytes 28
  9.1 5.7 %copy-start.40 = (f32[4,3,256]{2,0,1:T(4,128)S(1)}, f32[4,3,256]{2,0,1:T(4,128)}, u32[]{:S(2)}) copy-start(f32[4,3,256]{2,0,1:T(4,128)} %param.24) | copy-start | bytes 36868
  9.1 30.8 %all-to-all-start = ((bf16[4,512,512]{2,1,0:T(8,128)(2,1)}), bf16[4,512,512]{2,1,0:T(8,128)(2,1)S(1)}, u32[]{:S(2)}, u32[]{:S(2)}) async-start(bf16[4,512,512]{2,1,0:T(8,128)(2,1)} %stack.2), calls=%async_computation | async-start | bytes 4194304 | tf_op jit(solution)/shard_map/all_to_all | solution.py:167
  13.6 136.5 %all-gather.11.cloned.1.call-start = ((), (), s32[]{:S(2)}) async-start(), calls=%async_computation.4 | async-start | bytes 1179648 | tf_op jit(solution)/shard_map/all_gather | solution.py:30
  39.9 1.3 copy-start.1
  41.2 5.6 %copy-start.3 = (bf16[4,64,8,512]{3,2,0,1:T(8,128)(2,1)}, bf16[4,64,8,512]{3,2,0,1:T(8,128)(2,1)S(1)}, u32[]{:S(2)}) copy-start(bf16[4,64,8,512]{3,2,0,1:T(8,128)(2,1)S(1)} %copy.70) | copy-start | bytes 6291460
  41.2 2.0 copy-start.51
  42.0 2.8 %copy-start.34 = (f32[512,256]{1,0:T(8,128)}, f32[512,256]{1,0:T(8,128)S(1)}, u32[]{:S(2)}) copy-start(f32[512,256]{1,0:T(8,128)S(1)} %fusion.183) | copy-start | bytes 1572868
  42.0 2.0 copy-start.52
  43.9 2.8 %copy-start.41 = (bf16[2048,2]{0,1:T(2,128)(2,1)S(1)}, bf16[2048,2]{0,1:T(2,128)(2,1)}, u32[]{:S(2)}) copy-start(bf16[2048,2]{0,1:T(2,128)(2,1)} %param.23) | copy-start | bytes 24580
  43.9 2.8 %copy-start.48 = (f32[2]{0:T(128)S(1)}, f32[2]{0:T(128)}, u32[]{:S(2)}) copy-start(f32[2]{0:T(128)} %param.27) | copy-start | bytes 28
  44.0 2.8 %copy-start.50 = (f32[2]{0:T(128)S(1)}, f32[2]{0:T(128)}, u32[]{:S(2)}) copy-start(f32[2]{0:T(128)} %exponential_negate_fusion) | copy-start | bytes 28
  44.0 5.4 %copy-start.42 = (bf16[2048,2]{0,1:T(2,128)(2,1)S(1)}, bf16[2048,2]{0,1:T(2,128)(2,1)}, u32[]{:S(2)}) copy-start(bf16[2048,2]{0,1:T(2,128)(2,1)} %param.22) | copy-start | bytes 24580
  44.0 5.4 %copy-start.49 = (f32[2]{0:T(128)S(1)}, f32[2]{0:T(128)}, u32[]{:S(2)}) copy-start(f32[2]{0:T(128)} %param.26) | copy-start | bytes 28
  44.8 6.9 %copy-start.36 = (f32[512,256]{1,0:T(8,128)}, f32[512,256]{1,0:T(8,128)S(1)}, u32[]{:S(2)}) copy-start(f32[512,256]{1,0:T(8,128)S(1)} %fusion.185) | copy-start | bytes 1572868
  44.8 7.0 %copy-start.44 = (f32[1,1,256]{2,0,1:T(1,128)S(1)}, f32[1,1,256]{2,0,1:T(1,128)}, u32[]{:S(2)}) copy-start(f32[1,1,256]{2,0,1:T(1,128)} %get-tuple-element.107) | copy-start | bytes 3076
  44.8 7.0 %copy-start.45 = (f32[1,1,256]{2,0,1:T(1,128)S(1)}, f32[1,1,256]{2,0,1:T(1,128)}, u32[]{:S(2)}) copy-start(f32[1,1,256]{2,0,1:T(1,128)} %get-tuple-element.108) | copy-start | bytes 3076
  44.8 7.0 %copy-start.46 = (f32[1,1,256]{2,0,1:T(1,128)S(1)}, f32[1,1,256]{2,0,1:T(1,128)}, u32[]{:S(2)}) copy-start(f32[1,1,256]{2,0,1:T(1,128)} %get-tuple-element.109) | copy-start | bytes 3076
  44.8 7.0 %copy-start.47 = (f32[1,1,256]{2,0,1:T(1,128)S(1)}, f32[1,1,256]{2,0,1:T(1,128)}, u32[]{:S(2)}) copy-start(f32[1,1,256]{2,0,1:T(1,128)} %get-tuple-element.110) | copy-start | bytes 3076
  44.8 7.0 %collective-permute-start = (f32[3,768]{1,0:T(4,128)S(1)}, f32[3,768]{1,0:T(4,128)S(1)}, u32[]{:S(2)}, u32[]{:S(2)}) collective-permute-start(f32[3,768]{1,0:T(4,128)S(1)} %pad_maximum_fusion.3), channel_id=1, source_target_pairs={{0,4},{4,8},{8,12},{12,16},{16,20},{20,24},{24,28},{28,32},{32,36}... | collective-permute-start | bytes 27656 | tf_op jit(solution)/shard_map/ppermute | solution.py:16
  53.5 19.6 %copy-start.7 = (f32[4,128,2,128]{3,2,1,0:T(2,128)}, f32[4,128,2,128]{3,2,1,0:T(2,128)S(1)}, u32[]{:S(2)}) copy-start(f32[4,128,2,128]{3,2,1,0:T(2,128)S(1)} %reshape.144) | copy-start | bytes 1572868
  63.1 2.7 %copy-start.35 = (f32[512,256]{1,0:T(8,128)S(1)}, f32[512,256]{1,0:T(8,128)}, u32[]{:S(2)}) copy-start(f32[512,256]{1,0:T(8,128)} %copy-done.34) | copy-start | bytes 1572868
  63.1 2.7 %copy-start.37 = (f32[512,256]{1,0:T(8,128)S(1)}, f32[512,256]{1,0:T(8,128)}, u32[]{:S(2)}) copy-start(f32[512,256]{1,0:T(8,128)} %copy-done.36) | copy-start | bytes 1572868
  63.1 2.7 %copy-start.43 = (f32[1,1,256]{2,0,1:T(1,128)S(1)}, f32[1,1,256]{2,0,1:T(1,128)}, u32[]{:S(2)}) copy-start(f32[1,1,256]{2,0,1:T(1,128)} %get-tuple-element.116) | copy-start | bytes 3076
  71.8 2.7 %copy-start.5 = (f32[4,2,128,256]{3,2,1,0:T(8,128)}, f32[4,2,128,256]{3,2,1,0:T(8,128)S(1)}, u32[]{:S(2)}) copy-start(f32[4,2,128,256]{3,2,1,0:T(8,128)S(1)} %fusion.26) | copy-start | bytes 3145732
  77.0 19.9 %copy-start.4 = (f32[4,2,128,128]{3,2,1,0:T(8,128)}, f32[4,2,128,128]{3,2,1,0:T(8,128)S(1)}, u32[]{:S(2)}) copy-start(f32[4,2,128,128]{3,2,1,0:T(8,128)S(1)} %get-tuple-element.276) | copy-start | bytes 1572868
  77.0 32.9 %copy-start.10 = (f32[4,2,128,128]{3,2,1,0:T(8,128)}, f32[4,2,128,128]{3,2,1,0:T(8,128)S(1)}, u32[]{:S(2)}) copy-start(f32[4,2,128,128]{3,2,1,0:T(8,128)S(1)} %get-tuple-element.280) | copy-start | bytes 1572868
  82.6 27.9 %copy-start.15 = (f32[2,128,128]{2,1,0:T(8,128)}, f32[2,128,128]{2,1,0:T(8,128)S(1)}, u32[]{:S(2)}) copy-start(f32[2,128,128]{2,1,0:T(8,128)S(1)} %fusion.140) | copy-start | bytes 393220
  97.1 15.6 %copy-start.17 = (f32[2,128,128]{2,1,0:T(8,128)}, f32[2,128,128]{2,1,0:T(8,128)S(1)}, u32[]{:S(2)}) copy-start(f32[2,128,128]{2,1,0:T(8,128)S(1)} %fusion.192) | copy-start | bytes 393220
  110.2 0.6 copy-start.21
  110.5 0.7 copy-start.23
  111.1 2.8 %copy-start.25 = (f32[2,128,128]{2,1,0:T(8,128)}, f32[2,128,128]{2,1,0:T(8,128)S(1)}, u32[]{:S(2)}) copy-start(f32[2,128,128]{2,1,0:T(8,128)S(1)} %convolution_add_fusion.11) | copy-start | bytes 393220
  112.1 76.5 %all-gather.9.cloned.1.call-start = ((), (), s32[]{:S(2)}) async-start(), calls=%async_computation.3 | async-start | bytes 1179648 | tf_op jit(solution)/shard_map/all_gather | solution.py:30
  112.4 1.5 copy-start.27
  112.7 1.2 copy-start.29
  113.0 0.9 copy-start.31
  116.8 7.0 %copy-start.2 = (bf16[4,512,512]{2,1,0:T(8,128)(2,1)S(1)}, bf16[4,512,512]{2,1,0:T(8,128)(2,1)}, u32[]{:S(2)}) copy-start(bf16[4,512,512]{2,1,0:T(8,128)(2,1)} %copy-done.1) | copy-start | bytes 6291460
  116.8 93.7 %all-to-all-start.2 = ((bf16[256,4,512]{2,0,1:T(8,128)(2,1)}), bf16[256,4,512]{2,0,1:T(8,128)(2,1)}, u32[]{:S(2)}, u32[]{:S(2)}) async-start(bf16[256,4,512]{2,0,1:T(8,128)(2,1)} %copy.66), calls=%async_computation.2 | async-start | bytes 2097152 | tf_op jit(solution)/shard_map/all_to_all | solution.py:238
  126.7 4.5 %copy-start.12 = (f32[512,256]{1,0:T(8,128)S(1)}, f32[512,256]{1,0:T(8,128)}, u32[]{:S(2)}) copy-start(f32[512,256]{1,0:T(8,128)} %get-tuple-element.101) | copy-start | bytes 1572868
  131.3 6.3 %copy-start.11 = (f32[512,256]{1,0:T(8,128)S(1)}, f32[512,256]{1,0:T(8,128)}, u32[]{:S(2)}) copy-start(f32[512,256]{1,0:T(8,128)} %get-tuple-element.102) | copy-start | bytes 1572868
  131.3 7.4 %copy-start.8 = (f32[4,128,2,128]{3,2,1,0:T(2,128)S(1)}, f32[4,128,2,128]{3,2,1,0:T(2,128)}, u32[]{:S(2)}) copy-start(f32[4,128,2,128]{3,2,1,0:T(2,128)} %copy-done.7) | copy-start | bytes 1572868
  132.3 8.9 %copy-start.6 = (f32[4,2,128,256]{3,2,1,0:T(8,128)S(1)}, f32[4,2,128,256]{3,2,1,0:T(8,128)}, u32[]{:S(2)}) copy-start(f32[4,2,128,256]{3,2,1,0:T(8,128)} %copy-done.5) | copy-start | bytes 3145732
  138.6 3.3 %copy-start.16 = (f32[2,128,128]{2,1,0:T(8,128)S(1)}, f32[2,128,128]{2,1,0:T(8,128)}, u32[]{:S(2)}) copy-start(f32[2,128,128]{2,1,0:T(8,128)} %copy-done.15) | copy-start | bytes 393220
  138.6 3.3 %copy-start.18 = (f32[2,128,128]{2,1,0:T(8,128)S(1)}, f32[2,128,128]{2,1,0:T(8,128)}, u32[]{:S(2)}) copy-start(f32[2,128,128]{2,1,0:T(8,128)} %copy-done.17) | copy-start | bytes 393220
  138.6 3.6 %copy-start.19 = (f32[2,128,128]{2,1,0:T(8,128)S(1)}, f32[2,128,128]{2,1,0:T(8,128)}, u32[]{:S(2)}) copy-start(f32[2,128,128]{2,1,0:T(8,128)} %convolution_add_fusion.10) | copy-start | bytes 393220
  138.6 3.6 %copy-start.22 = (f32[2,128,128]{2,1,0:T(8,128)S(1)}, f32[2,128,128]{2,1,0:T(8,128)}, u32[]{:S(2)}) copy-start(f32[2,128,128]{2,1,0:T(8,128)} %copy-done.21) | copy-start | bytes 393220
  138.6 3.6 %copy-start.24 = (f32[2,128,128]{2,1,0:T(8,128)S(1)}, f32[2,128,128]{2,1,0:T(8,128)}, u32[]{:S(2)}) copy-start(f32[2,128,128]{2,1,0:T(8,128)} %copy-done.23) | copy-start | bytes 393220
  138.6 3.6 %copy-start.26 = (f32[2,128,128]{2,1,0:T(8,128)S(1)}, f32[2,128,128]{2,1,0:T(8,128)}, u32[]{:S(2)}) copy-start(f32[2,128,128]{2,1,0:T(8,128)} %copy-done.25) | copy-start | bytes 393220
  138.7 4.5 %copy-start.20 = (f32[2,128,128]{2,1,0:T(8,128)S(1)}, f32[2,128,128]{2,1,0:T(8,128)}, u32[]{:S(2)}) copy-start(f32[2,128,128]{2,1,0:T(8,128)} %fusion.195) | copy-start | bytes 393220
  138.7 4.5 %copy-start.28 = (f32[2,128,128]{2,1,0:T(8,128)S(1)}, f32[2,128,128]{2,1,0:T(8,128)}, u32[]{:S(2)}) copy-start(f32[2,128,128]{2,1,0:T(8,128)} %copy-done.27) | copy-start | bytes 393220
  138.7 4.5 %copy-start.30 = (f32[2,128,128]{2,1,0:T(8,128)S(1)}, f32[2,128,128]{2,1,0:T(8,128)}, u32[]{:S(2)}) copy-start(f32[2,128,128]{2,1,0:T(8,128)} %copy-done.29) | copy-start | bytes 393220
  138.7 4.5 %copy-start.32 = (f32[2,128,128]{2,1,0:T(8,128)S(1)}, f32[2,128,128]{2,1,0:T(8,128)}, u32[]{:S(2)}) copy-start(f32[2,128,128]{2,1,0:T(8,128)} %copy-done.31) | copy-start | bytes 393220
  188.6 3.9 %copy-start.9 = (f32[16,128,128]{2,1,0:T(8,128)S(1)}, f32[16,128,128]{2,1,0:T(8,128)}, u32[]{:S(2)}) copy-start(f32[16,128,128]{2,1,0:T(8,128)} %all-gather.9.cloned.1.call-done) | copy-start | bytes 3145732
  188.6 5.1 %copy-start.33 = (f32[16,128,128]{2,1,0:T(8,128)S(1)}, f32[16,128,128]{2,1,0:T(8,128)}, u32[]{:S(2)}) copy-start(f32[16,128,128]{2,1,0:T(8,128)} %all-gather.11.cloned.1.call-done) | copy-start | bytes 3145732
  192.5 2.3 copy-start.38
  193.7 1.4 copy-start.39
  195.4 7.8 %copy-start.13 = (f32[4,128,2,128]{3,2,1,0:T(2,128)S(1)}, f32[4,128,2,128]{3,2,1,0:T(2,128)}, u32[]{:S(2)}) copy-start(f32[4,128,2,128]{3,2,1,0:T(2,128)} %reshape.143) | copy-start | bytes 1572868
  203.2 4.9 %copy-start.54 = (f32[128]{0:T(128)S(1)}, f32[128]{0:T(128)}, u32[]{:S(2)}) copy-start(f32[128]{0:T(128)} %param.28) | copy-start | bytes 1540
  205.2 2.9 %copy-start.14 = (bf16[512,2048,1]{1,0,2:T(8,128)(2,1)S(1)}, bf16[512,2048,1]{1,0,2:T(8,128)(2,1)}, u32[]{:S(2)}) copy-start(bf16[512,2048,1]{1,0,2:T(8,128)(2,1)} %reshape.209) | copy-start | bytes 6291460
Sparse Core Ops, SparseCore 0:
  112.2 37.7 all-gather.10
  151.8 36.7 all-gather.8
